TPU v7x, 32 devices: a whole 2x2x4 slice. The times are simulated.
32 devices in a mesh: dp: 4 (over y, x), expert: 8 (over z, core).
Axes of the slice: x: 2, y: 2, z: 4, core: 2. Of those that a mesh axis runs over, the one named last changes fastest.
Arguments:
- master: float32 [2, 32, 64, 2880], P(None, 'expert', 'dp'), may hold values from -6 to 6
- moment_one: float32 [2, 32, 64, 2880], P(None, 'expert', 'dp'), may hold values from -1.2 to 1.2
- moment_two: float32 [2, 32, 64, 2880], P(None, 'expert', 'dp'), may hold values from 0.0005 to 0.5
- gradient: bfloat16 [2, 32, 64, 2880], P(None, 'expert', 'dp'), may hold values from -150000 to 150000
- old_slot: int32 [2, 32], replicated, may hold values from 0 to 31, as said below
- new_slot: int32 [2, 32], replicated, may hold values from 0 to 31, as said below
Outputs:
- new_master: float32 [2, 32, 64, 2880], P(None, 'expert', 'dp')
- new_moment_one: float32 [2, 32, 64, 2880], P(None, 'expert', 'dp')
- new_moment_two: float32 [2, 32, 64, 2880], P(None, 'expert', 'dp')
Inputs may be any that keep to these rules, and one draw needn't show every extreme that they name: `old_slot`: for each layer a permutation of 0 to 31; global slot s is held by index s // 4 of expert. `new_slot`: for each layer a permutation of 0 to 31; in each layer exactly 1 slot of each index of expert receives another expert than it held, and exactly 1 of the experts held by each index leaves its slot; all other experts keep their slot.
All inputs are finite; a program needn't handle non-finite values.
Results may differ from a plain program's by a relative error of at most 0.001.
Values sent between devices are 32-bit elements; how exact they have to be, the bound alone decides.
A program may use at most 64 MiB of HBM per device.

v0:
```python
import math

import jax
import jax.numpy as jnp
from jax import lax
from jax.sharding import PartitionSpec as P

MOVE_DEV = 1


BETA_ONE = 0.9
BETA_TWO = 0.95
LEARN_RATE = 0.05
DECAY_RATE = 0.1
ADAM_EPS = 1e-08
CLIP_RMS = 2.0
FIRST_FIX = 1.0 - 0.9**10
SECOND_FIX = 1.0 - 0.95**10


def adam_update(master, moment_one, moment_two, gradient, clip_scale):
    scaled = gradient * clip_scale
    first_moment = BETA_ONE * moment_one + (1.0 - BETA_ONE) * scaled
    second = BETA_TWO * moment_two + (1.0 - BETA_TWO) * scaled * scaled
    step_dir = first_moment / FIRST_FIX / (jnp.sqrt(second / SECOND_FIX) + ADAM_EPS)
    weights = master - LEARN_RATE * (step_dir + DECAY_RATE * master)
    return (weights, first_moment, second)


def clip_factor(square_sum, entry_count):
    return jnp.minimum(1.0, CLIP_RMS * math.sqrt(entry_count) / (jnp.sqrt(square_sum) + 1e-06))


def grad_total(gradient):
    return lax.psum(jnp.sum(gradient * gradient), ("dp", "expert"))


def pick_rows(data, chosen):
    return jax.vmap(lambda layer_block, layer_pick: jnp.take(layer_block, layer_pick, axis=0))(
        data, chosen
    )


def build_plan(old_slot, new_slot, slot_count, group_size, my_index):
    layer_count = old_slot.shape[0]
    holder = jnp.argsort(new_slot, axis=1)
    resident = jnp.argsort(old_slot, axis=1)
    source = jnp.take_along_axis(old_slot, holder, axis=1)
    target = jnp.take_along_axis(new_slot, resident, axis=1)
    position = lax.broadcasted_iota(jnp.int32, source.shape, 1)
    leaving = target != position
    arriving = source != position
    capacity = MOVE_DEV
    shaped = (layer_count, group_size, slot_count)
    out_order = jnp.argsort(jnp.where(leaving, 0, 1).reshape(shaped), axis=2, stable=True)[
        :, :, :capacity
    ]
    in_order = jnp.argsort(jnp.where(arriving, 0, 1).reshape(shaped), axis=2, stable=True)[
        :, :, :capacity
    ]
    out_rank = (jnp.cumsum(leaving.astype(jnp.int32).reshape(shaped), axis=2) - 1).reshape(
        source.shape
    )
    in_rank = jnp.cumsum(arriving.astype(jnp.int32).reshape(shaped), axis=2) - 1
    device_base = lax.broadcasted_iota(jnp.int32, in_order.shape, 1) * slot_count
    wanted = (device_base + in_order).reshape(layer_count, group_size * capacity)
    anchor = jnp.take_along_axis(source, wanted, axis=1)
    sender = anchor // slot_count
    list_place = jnp.clip(jnp.take_along_axis(out_rank, anchor, axis=1), 0, capacity - 1)
    gather_index = (list_place * group_size + sender).reshape(layer_count, group_size, capacity)
    gather_index = jnp.transpose(gather_index, (0, 2, 1)).reshape(
        layer_count, capacity * group_size
    )
    my_out = lax.dynamic_index_in_dim(out_order, my_index, axis=1, keepdims=False)
    my_arrive = lax.dynamic_index_in_dim(arriving.reshape(shaped), my_index, axis=1, keepdims=False)
    my_rank = jnp.clip(
        lax.dynamic_index_in_dim(in_rank, my_index, axis=1, keepdims=False), 0, capacity - 1
    )
    return (capacity, my_out, gather_index, my_arrive, my_rank)


def relocate(arrays, route_plan, group_size):
    capacity, my_out, gather_index, my_arrive, my_rank = route_plan
    layer_count, slot_count, row_count, col_count = arrays[0].shape
    flat_size = row_count * col_count
    piece_size = flat_size // group_size
    packed = tuple(
        (
            pick_rows(member.reshape(layer_count, slot_count, flat_size), my_out).reshape(
                layer_count, capacity, group_size, piece_size
            )
            for member in arrays
        )
    )
    spread = lax.all_to_all(packed, "expert", split_axis=2, concat_axis=2, tiled=True)
    regrouped = tuple(
        (
            pick_rows(
                member.reshape(layer_count, capacity * group_size, piece_size), gather_index
            ).reshape(layer_count, capacity, group_size, piece_size)
            for member in spread
        )
    )
    landed = lax.all_to_all(regrouped, "expert", split_axis=2, concat_axis=2, tiled=True)
    results = []
    for member, initial in zip(landed, arrays):
        arrived = pick_rows(member.reshape(layer_count, capacity, flat_size), my_rank).reshape(
            initial.shape
        )
        results.append(jnp.where(my_arrive[:, :, None, None], arrived, initial))
    return tuple(results)


def shards(master, moment_one, moment_two, gradient, old_slot, new_slot):
    layer_count, slot_count, row_count, col_count = master.shape
    group_size = lax.axis_size("expert")
    entry_count = (
        layer_count * slot_count * group_size * row_count * lax.axis_size("dp") * col_count
    )
    my_index = lax.axis_index("expert")
    route_plan = build_plan(old_slot, new_slot, slot_count, group_size, my_index)
    moved = relocate(
        (master, moment_one, moment_two, gradient.astype(jnp.float32)), route_plan, group_size
    )
    clip_scale = clip_factor(grad_total(moved[3]), entry_count)
    return adam_update(moved[0], moved[1], moved[2], moved[3], clip_scale)


def solution(mesh):
    in_specs = (
        P(None, "expert", "dp", None),
        P(None, "expert", "dp", None),
        P(None, "expert", "dp", None),
        P(None, "expert", "dp", None),
        P(),
        P(),
    )
    out_specs = (
        P(None, "expert", "dp", None),
        P(None, "expert", "dp", None),
        P(None, "expert", "dp", None),
    )
    return jax.shard_map(shards, mesh=mesh, in_specs=in_specs, out_specs=out_specs, check_vma=False)
```

profile of v0, /device:TPU:0, one launch (start us, length us, event | category | flops | bytes accessed | tf_op | source)
XLA Modules:
  0.0 239.6 jit_solution(1866940391508601473)
XLA Ops:
  0.6 0.8 copy.70
  1.4 0.8 copy.65
  2.2 0.8 sort.63
  3.0 0.8 sort.62
  4.0 1.6 gather_fusion.1
  5.8 0.1 copy.75
  5.9 0.7 sort.64
  6.5 0.2 dynamic-slice_reduce_fusion
  6.8 2.3 reshape.178
  9.1 2.3 reshape.190
  11.5 2.0 gather_fusion.2
  13.5 2.7 %gather_fusion.7 = f32[2,46080]{1,0:T(2,128)} fusion(f32[2,4,46080]{2,1,0:T(4,128)S(1)} %reshape.190, s32[2]{0:T(128)S(1)} %or_bitcast_fusion), kind=kCustom, calls=%fused_computation.6.clone | custom fusion | bytes 737296 | tf_op jit(solution)/shard_map/vmap(jit(_take))/gather | solution.py:39
  16.2 1.2 reshape.202
  17.4 2.7 %gather_fusion.13 = f32[2,46080]{1,0:T(2,128)} fusion(f32[2,4,46080]{2,1,0:T(4,128)S(1)} %reshape.202, s32[2]{0:T(128)S(1)} %or_bitcast_fusion), kind=kCustom, calls=%fused_computation.8.clone | custom fusion | bytes 737296 | tf_op jit(solution)/shard_map/vmap(jit(_take))/gather | solution.py:39
  20.1 1.1 reshape.196
  21.2 2.7 %gather_fusion.10 = f32[2,46080]{1,0:T(2,128)} fusion(f32[2,4,46080]{2,1,0:T(4,128)S(1)} %reshape.196, s32[2]{0:T(128)S(1)} %or_bitcast_fusion), kind=kCustom, calls=%fused_computation.7.clone | custom fusion | bytes 737296 | tf_op jit(solution)/shard_map/vmap(jit(_take))/gather | solution.py:39
  23.9 2.7 %bitcast_select_fusion = (f32[2,1,46080]{2,0,1:T(2,128)}, f32[2,1,46080]{2,0,1:T(2,128)S(1)}, f32[2,1,46080]{2,0,1:T(2,128)}, f32[2,1,46080]{2,0,1:T(2,128)}) fusion(f32[2,46080]{1,0:T(2,128)} %gather_fusion.13, pred[2]{0:T(512)(128)(4,1)S(1)} %and_bitcast_fusion, f32[2,46080]{1,0:T(2,128)S(1)} %copy-done.4, f32[2,46080]{1,0:T(2,128)} %gather_fusion.10, ...), kind=kLoop, calls=%fused_computation.26 | loop fusion | flops 368640 | bytes 2949122 | tf_op jit(solution)/shard_map/vmap(jit(_take))/select_n | solution.py:39
  26.6 18.1 %all_to_all.40 = f32[2,1,8,5760]{3,0,1,2:T(2,128)S(1)} all-to-all(f32[2,1,8,5760]{3,0,1,2:T(2,128)S(1)} %bitcast.111), channel_id=1, replica_groups=mesh['dp'=4,'expert'=8] {'expert'}, dimensions={2} | all-to-all | bytes 737280 | tf_op jit(solution)/shard_map/all_to_all | solution.py:95
  44.7 3.4 %all-to-all-start.6 = ((f32[2,1,8,5760]{3,0,1,2:T(2,128)}), f32[2,1,8,5760]{3,0,1,2:T(2,128)S(1)}, u32[]{:S(2)}, u32[]{:S(2)}) async-start(f32[2,1,8,5760]{3,0,1,2:T(2,128)} %bitcast.28), calls=%async_computation.6 | async-start | bytes 737280 | tf_op jit(solution)/shard_map/all_to_all | solution.py:95
  48.3 0.9 gather_fusion
  49.3 0.1 copy.69
  49.4 0.7 sort.65
  50.1 10.0 %all-to-all-done.6 = f32[2,1,8,5760]{3,0,1,2:T(2,128)S(1)} async-done(((f32[2,1,8,5760]{3,0,1,2:T(2,128)}), f32[2,1,8,5760]{3,0,1,2:T(2,128)S(1)}, u32[]{:S(2)}, u32[]{:S(2)}) %all-to-all-start.6) | async-done | bytes 368672 | tf_op jit(solution)/shard_map/all_to_all | solution.py:95
  60.1 3.4 %all-to-all-start.4 = ((f32[2,1,8,5760]{3,0,1,2:T(2,128)}), f32[2,1,8,5760]{3,0,1,2:T(2,128)S(1)}, u32[]{:S(2)}, u32[]{:S(2)}) async-start(f32[2,1,8,5760]{3,0,1,2:T(2,128)} %bitcast.23), calls=%async_computation.4 | async-start | bytes 737280 | tf_op jit(solution)/shard_map/all_to_all | solution.py:95
  63.7 0.7 gather_fusion.3
  64.6 0.3 reduce_window_sum.17
  64.9 10.5 %all-to-all-done.4 = f32[2,1,8,5760]{3,0,1,2:T(2,128)S(1)} async-done(((f32[2,1,8,5760]{3,0,1,2:T(2,128)}), f32[2,1,8,5760]{3,0,1,2:T(2,128)S(1)}, u32[]{:S(2)}, u32[]{:S(2)}) %all-to-all-start.4) | async-done | bytes 368672 | tf_op jit(solution)/shard_map/all_to_all | solution.py:95
  75.5 3.6 %all-to-all-start = ((f32[2,1,8,5760]{3,0,1,2:T(2,128)}), f32[2,1,8,5760]{3,0,1,2:T(2,128)S(1)}, u32[]{:S(2)}, u32[]{:S(2)}) async-start(f32[2,1,8,5760]{3,0,1,2:T(2,128)} %bitcast.11), calls=%async_computation | async-start | bytes 737280 | tf_op jit(solution)/shard_map/all_to_all | solution.py:95
  79.2 0.7 gather_fusion.4
  80.0 0.1 copy.74
  80.2 0.8 gather_fusion.8
  81.1 0.8 gather_fusion.14
  82.0 0.8 gather_fusion.11
  82.8 8.0 %all-to-all-done = f32[2,1,8,5760]{3,0,1,2:T(2,128)S(1)} async-done(((f32[2,1,8,5760]{3,0,1,2:T(2,128)}), f32[2,1,8,5760]{3,0,1,2:T(2,128)S(1)}, u32[]{:S(2)}, u32[]{:S(2)}) %all-to-all-start) | async-done | bytes 368672 | tf_op jit(solution)/shard_map/all_to_all | solution.py:95
  90.9 0.8 gather_fusion.5
  91.7 1.7 fusion.1
  93.4 14.4 %all_to_all.41 = f32[2,1,8,5760]{3,0,1,2:T(2,128)S(1)} all-to-all(f32[2,1,8,5760]{3,0,1,2:T(2,128)S(1)} %get-tuple-element.26), channel_id=1, replica_groups=mesh['dp'=4,'expert'=8] {'expert'}, dimensions={2} | all-to-all | bytes 737280 | tf_op jit(solution)/shard_map/all_to_all | solution.py:104
  107.8 14.4 %all_to_all.42 = f32[2,1,8,5760]{3,0,1,2:T(2,128)S(1)} all-to-all(f32[2,1,8,5760]{3,0,1,2:T(2,128)S(1)} %get-tuple-element.27), channel_id=1, replica_groups=mesh['dp'=4,'expert'=8] {'expert'}, dimensions={2} | all-to-all | bytes 737280 | tf_op jit(solution)/shard_map/all_to_all | solution.py:104
  122.1 3.4 %all-to-all-start.5 = ((f32[2,1,8,5760]{3,0,1,2:T(2,128)}), f32[2,1,8,5760]{3,0,1,2:T(2,128)S(1)}, u32[]{:S(2)}, u32[]{:S(2)}) async-start(f32[2,1,8,5760]{3,0,1,2:T(2,128)} %get-tuple-element.28), calls=%async_computation.5 | async-start | bytes 737280 | tf_op jit(solution)/shard_map/all_to_all | solution.py:104
  125.6 0.1 reshape.177
  125.7 11.8 %all-to-all-done.5 = f32[2,1,8,5760]{3,0,1,2:T(2,128)S(1)} async-done(((f32[2,1,8,5760]{3,0,1,2:T(2,128)}), f32[2,1,8,5760]{3,0,1,2:T(2,128)S(1)}, u32[]{:S(2)}, u32[]{:S(2)}) %all-to-all-start.5) | async-done | bytes 368672 | tf_op jit(solution)/shard_map/all_to_all | solution.py:104
  137.5 3.4 %all-to-all-start.1 = ((f32[2,1,8,5760]{3,0,1,2:T(2,128)}), f32[2,1,8,5760]{3,0,1,2:T(2,128)S(1)}, u32[]{:S(2)}, u32[]{:S(2)}) async-start(f32[2,1,8,5760]{3,0,1,2:T(2,128)} %get-tuple-element.29), calls=%async_computation.1 | async-start | bytes 737280 | tf_op jit(solution)/shard_map/all_to_all | solution.py:104
  141.0 0.3 reduce_window_sum.18
  141.5 0.3 reshape.206
  141.9 0.3 reshape.194
  142.3 0.3 reshape.200
  142.6 10.3 %all-to-all-done.1 = f32[2,1,8,5760]{3,0,1,2:T(2,128)S(1)} async-done(((f32[2,1,8,5760]{3,0,1,2:T(2,128)}), f32[2,1,8,5760]{3,0,1,2:T(2,128)S(1)}, u32[]{:S(2)}, u32[]{:S(2)}) %all-to-all-start.1) | async-done | bytes 368672 | tf_op jit(solution)/shard_map/all_to_all | solution.py:104
  152.9 0.3 reshape.187
  153.3 2.8 %gather_fusion.6 = f32[8,46080]{1,0:T(8,128)} fusion(f32[2,1,46080]{2,1,0:T(1,128)S(1)} %reshape.187, s32[8]{0:T(128)S(1)} %reshape.407), kind=kCustom, calls=%fused_computation.4.clone | custom fusion | bytes 2949184 | tf_op jit(solution)/shard_map/vmap(jit(_take))/gather | solution.py:39
  156.0 2.9 %reshape.410 = f32[2,4,46080]{2,1,0:T(4,128)} reshape(f32[8,46080]{1,0:T(8,128)} %gather_fusion.6) | data formatting | bytes 2949120 | tf_op jit(solution)/shard_map/vmap(jit(_take))/gather | solution.py:39
  159.0 2.8 %gather_fusion.12 = f32[8,46080]{1,0:T(8,128)} fusion(f32[2,1,46080]{2,1,0:T(1,128)S(1)} %reshape.200, s32[8]{0:T(128)S(1)} %reshape.407), kind=kCustom, calls=%fused_computation.14.clone | custom fusion | bytes 2949184 | tf_op jit(solution)/shard_map/vmap(jit(_take))/gather | solution.py:39
  161.7 2.9 %reshape.440 = f32[2,4,46080]{2,1,0:T(4,128)} reshape(f32[8,46080]{1,0:T(8,128)} %gather_fusion.12) | data formatting | bytes 2949120 | tf_op jit(solution)/shard_map/vmap(jit(_take))/gather | solution.py:39
  164.7 2.8 %gather_fusion.9 = f32[8,46080]{1,0:T(8,128)} fusion(f32[2,1,46080]{2,1,0:T(1,128)S(1)} %reshape.194, s32[8]{0:T(128)S(1)} %reshape.407), kind=kCustom, calls=%fused_computation.13.clone | custom fusion | bytes 2949184 | tf_op jit(solution)/shard_map/vmap(jit(_take))/gather | solution.py:39
  167.4 2.9 %reshape.425 = f32[2,4,46080]{2,1,0:T(4,128)} reshape(f32[8,46080]{1,0:T(8,128)} %gather_fusion.9) | data formatting | bytes 2949120 | tf_op jit(solution)/shard_map/vmap(jit(_take))/gather | solution.py:39
  170.3 2.8 %gather_fusion.15 = f32[8,46080]{1,0:T(8,128)} fusion(f32[2,1,46080]{2,1,0:T(1,128)S(1)} %reshape.206, s32[8]{0:T(128)S(1)} %reshape.407), kind=kCustom, calls=%fused_computation.15.clone | custom fusion | bytes 2949184 | tf_op jit(solution)/shard_map/vmap(jit(_take))/gather | solution.py:39
  173.1 3.0 %reshape.455 = f32[2,4,46080]{2,1,0:T(4,128)} reshape(f32[8,46080]{1,0:T(8,128)} %gather_fusion.15) | data formatting | bytes 2949120 | tf_op jit(solution)/shard_map/vmap(jit(_take))/gather | solution.py:39
  176.1 5.8 %broadcast_select_fusion.1 = (f32[2,4,46080]{2,1,0:T(4,128)}, f32[2,4,46080]{2,1,0:T(4,128)}, f32[2,4,46080]{2,1,0:T(4,128)}, f32[2,4,46080]{2,1,0:T(4,128)}) fusion(f32[2,4,46080]{2,1,0:T(4,128)} %reshape.455, pred[2,4]{1,0:T(4,128)(4,1)S(1)} %compare_and_fusion, f32[2,4,46080]{2,1,0:T(4,128)} %reshape.425, f32[2,4,46080]{2,1,0:T(4,128)} %reshape.440, ...), kind=kLoop, calls=%fused_computation.22 | loop fusion | flops 1474560 | bytes 11796488 | tf_op jit(solution)/shard_map/vmap(jit(_take))/select_n | solution.py:39
  181.9 2.0 reshape.201
  183.9 1.1 multiply_reduce_fusion
  185.0 2.8 %reshape.207 = f32[2,4,16,2880]{3,2,1,0:T(8,128)} reshape(f32[2,4,46080]{2,1,0:T(4,128)} %get-tuple-element.30) | data formatting | bytes 2949120 | tf_op jit(solution)/shard_map/reshape | solution.py:107
  187.8 38.7 %psum.7 = f32[]{:T(128)} all-reduce(f32[]{:T(128)} %multiply_reduce_fusion), channel_id=1, replica_groups=mesh['dp'=4,'expert'=8] {'dp','expert'}, use_global_device_ids=true, to_apply=%region_7.13 | all-reduce | flops 1 | bytes 8 | tf_op jit(solution)/shard_map/psum | solution.py:35
  227.2 2.8 %reshape.195 = f32[2,4,16,2880]{3,2,1,0:T(8,128)} reshape(f32[2,4,46080]{2,1,0:T(4,128)} %get-tuple-element.31) | data formatting | bytes 2949120 | tf_op jit(solution)/shard_map/reshape | solution.py:107
  230.0 2.8 %reshape.189 = f32[2,4,16,2880]{3,2,1,0:T(8,128)} reshape(f32[2,4,46080]{2,1,0:T(4,128)} %get-tuple-element.33) | data formatting | bytes 2949120 | tf_op jit(solution)/shard_map/reshape | solution.py:107
  232.9 6.8 %multiply_subtract_fusion = (f32[2,4,16,2880]{3,2,1,0:T(8,128)}, f32[2,4,16,2880]{3,2,1,0:T(8,128)}, f32[2,4,16,2880]{3,2,1,0:T(8,128)}) fusion(f32[2,4,16,2880]{3,2,1,0:T(8,128)} %reshape.189, f32[2,4,16,2880]{3,2,1,0:T(8,128)} %param.16, pred[2,4]{1,0:T(4,128)(4,1)S(1)} %bitcast.118, f32[]{:T(128)S(6)} %min_shard_map.3, ...), kind=kLoop, calls=%fused_computation.18 | loop fusion | flops 7741440 | bytes 15482892 | tf_op jit(solution)/shard_map/sub | solution.py:26
  (61 shorter events, 1.7 us)
Async XLA Ops:
  13.5 2.7 %copy-start.2 = (f32[2,4,16,2880]{3,2,1,0:T(8,128)S(1)}, f32[2,4,16,2880]{3,2,1,0:T(8,128)}, u32[]{:S(2)}) copy-start(f32[2,4,16,2880]{3,2,1,0:T(8,128)} %param.18) | copy-start | bytes 4423684
  17.4 2.7 %copy-start.1 = (bf16[2,4,16,2880]{3,2,1,0:T(8,128)(2,1)S(1)}, bf16[2,4,16,2880]{3,2,1,0:T(8,128)(2,1)}, u32[]{:S(2)}) copy-start(bf16[2,4,16,2880]{3,2,1,0:T(8,128)(2,1)} %param.19) | copy-start | bytes 2211844
  21.2 2.7 %copy-start.4 = (f32[2,46080]{1,0:T(2,128)S(1)}, f32[2,46080]{1,0:T(2,128)}, u32[]{:S(2)}) copy-start(f32[2,46080]{1,0:T(2,128)} %gather_fusion.7) | copy-start | bytes 1105924
  23.9 24.4 %copy-start = (s32[2,32]{1,0:T(2,128)S(1)}, s32[2,32]{1,0:T(2,128)}, u32[]{:S(2)}) copy-start(s32[2,32]{1,0:T(2,128)} %param.20) | copy-start | bytes 772
  44.7 15.4 %all-to-all-start.6 = ((f32[2,1,8,5760]{3,0,1,2:T(2,128)}), f32[2,1,8,5760]{3,0,1,2:T(2,128)S(1)}, u32[]{:S(2)}, u32[]{:S(2)}) async-start(f32[2,1,8,5760]{3,0,1,2:T(2,128)} %bitcast.28), calls=%async_computation.6 | async-start | bytes 737280 | tf_op jit(solution)/shard_map/all_to_all | solution.py:95
  60.1 15.4 %all-to-all-start.4 = ((f32[2,1,8,5760]{3,0,1,2:T(2,128)}), f32[2,1,8,5760]{3,0,1,2:T(2,128)S(1)}, u32[]{:S(2)}, u32[]{:S(2)}) async-start(f32[2,1,8,5760]{3,0,1,2:T(2,128)} %bitcast.23), calls=%async_computation.4 | async-start | bytes 737280 | tf_op jit(solution)/shard_map/all_to_all | solution.py:95
  75.5 15.4 %all-to-all-start = ((f32[2,1,8,5760]{3,0,1,2:T(2,128)}), f32[2,1,8,5760]{3,0,1,2:T(2,128)S(1)}, u32[]{:S(2)}, u32[]{:S(2)}) async-start(f32[2,1,8,5760]{3,0,1,2:T(2,128)} %bitcast.11), calls=%async_computation | async-start | bytes 737280 | tf_op jit(solution)/shard_map/all_to_all | solution.py:95
  122.1 15.4 %all-to-all-start.5 = ((f32[2,1,8,5760]{3,0,1,2:T(2,128)}), f32[2,1,8,5760]{3,0,1,2:T(2,128)S(1)}, u32[]{:S(2)}, u32[]{:S(2)}) async-start(f32[2,1,8,5760]{3,0,1,2:T(2,128)} %get-tuple-element.28), calls=%async_computation.5 | async-start | bytes 737280 | tf_op jit(solution)/shard_map/all_to_all | solution.py:104
  137.5 15.4 %all-to-all-start.1 = ((f32[2,1,8,5760]{3,0,1,2:T(2,128)}), f32[2,1,8,5760]{3,0,1,2:T(2,128)S(1)}, u32[]{:S(2)}, u32[]{:S(2)}) async-start(f32[2,1,8,5760]{3,0,1,2:T(2,128)} %get-tuple-element.29), calls=%async_computation.1 | async-start | bytes 737280 | tf_op jit(solution)/shard_map/all_to_all | solution.py:104
  173.1 3.0 %copy-start.3 = (f32[2,4,46080]{2,1,0:T(4,128)S(1)}, f32[2,4,46080]{2,1,0:T(4,128)}, u32[]{:S(2)}) copy-start(f32[2,4,46080]{2,1,0:T(4,128)} %reshape.410) | copy-start | bytes 4423684
where the time goes:
time: 241 us; the launch traced here: 240 us
  blocking collectives  85.5 us (35%)
  local copies, waits for them, and re-layouts  62.5 us (26%)
  waiting for transfers between devices  50.6 us (21%)
  other arithmetic  21.8 us (9%)
  starting transfers between devices  17.4 us (7%)
    psum x1, blocking collectives, grad_total(): return lax.psum(jnp.sum(gradient * gradient), ('dp', 'expert'))  38.7 us
    gather x18, local copies, waits for them, and re-layouts, pick_rows(): jnp.take(layer_block, layer_pick, axis=0)  36.5 us
    all_to_all x2, blocking collectives, relocate(): lax.all_to_all(regrouped, 'expert', split_axis=2, concat_axis=2, tiled=True)  28.7 us
    all_to_all x3, waiting for transfers between devices, relocate(): lax.all_to_all(packed, 'expert', split_axis=2, concat_axis=2, tiled=True)  28.6 us
    all_to_all x2, waiting for transfers between devices, relocate(): lax.all_to_all(regrouped, 'expert', split_axis=2, concat_axis=2, tiled=True)  22.1 us
    all_to_all x1, blocking collectives, relocate(): lax.all_to_all(packed, 'expert', split_axis=2, concat_axis=2, tiled=True)  18.1 us
    all_to_all x3, starting transfers between devices, relocate(): lax.all_to_all(packed, 'expert', split_axis=2, concat_axis=2, tiled=True)  10.5 us
    reshape x4, local copies, waits for them, and re-layouts, relocate(): pick_rows(member.reshape(layer_count, capacity, flat_size), my_rank)  10.5 us
  transfers between devices with their start and end apart: 5, of which 5 were waited for; matrix products, arithmetic and copies ran while one was open for 4% of the time, Pallas kernels for 0%

commit v1 on v0

v1 whole, which is shorter than its diff:
```python
import functools
import math

import jax
import jax.numpy as jnp
from jax import lax
from jax.experimental import pallas as pl
from jax.experimental.pallas import tpu as pltpu
from jax.sharding import PartitionSpec as P

MESH = pl.DeviceIdType.MESH
BETA_ONE = 0.9
BETA_TWO = 0.95
LEARN_RATE = 0.05
DECAY_RATE = 0.1
ADAM_EPS = 1e-08
CLIP_RMS = 2.0
FIRST_FIX = 1.0 - 0.9**10
SECOND_FIX = 1.0 - 0.95**10
SUB, LANE = 8, 128


def moments(moment_one, moment_two, gradient, clip_scale):
    scaled = gradient * clip_scale
    first_moment = BETA_ONE * moment_one + (1.0 - BETA_ONE) * scaled
    second = BETA_TWO * moment_two + (1.0 - BETA_TWO) * scaled * scaled
    return first_moment, second


def weights_of(master, first_moment, second):
    step_dir = first_moment / FIRST_FIX / (jnp.sqrt(second / SECOND_FIX) + ADAM_EPS)
    return master - LEARN_RATE * (step_dir + DECAY_RATE * master)


def plan_kernel(group, slots, old_ref, new_ref, mine_ref, send_ref, pick_ref, count_ref, dst_ref, src_ref, rank_ref):
    layers, experts = old_ref.shape
    half = group // 2
    me = lax.axis_index("expert")
    my_half = lax.div(me, half)

    def clear(i, c):
        send_ref[i] = 0
        return c

    lax.fori_loop(0, layers * half, clear, 0)
    for layer in range(layers):

        def expert_step(e, c):
            old, new = old_ref[layer, e], new_ref[layer, e]

            @pl.when(old != new)
            def _():
                src, dst = lax.div(old, slots), lax.div(new, slots)
                dst_ref[layer * group + src] = dst
                src_ref[layer * group + dst] = src

                @pl.when(src == me)
                def _():
                    mine_ref[layer] = lax.rem(old, slots)

                @pl.when(dst == me)
                def _():
                    mine_ref[layers + layer] = lax.rem(new, slots)

            return c

        lax.fori_loop(0, experts, expert_step, 0)
    counts = [jnp.int32(0), jnp.int32(0)]
    for layer in range(layers):
        for side in range(2):

            def rank_step(j, count, side=side):
                at = layer * group + side * half + j
                crosses = lax.div(dst_ref[at], half) != side
                rank_ref[at] = count

                @pl.when(crosses & (my_half == side))
                def _():
                    send_ref[count] = layer * half + j

                return count + crosses.astype(jnp.int32)

            counts[side] = lax.fori_loop(0, half, rank_step, counts[side])
    count_ref[0] = counts[0]
    for layer in range(layers):

        def pick_step(j, c):
            src = src_ref[layer * group + my_half * half + j]
            local = lax.div(src, half) == my_half
            pick_ref[layer * half + j] = jnp.where(
                local,
                layer * half + lax.rem(src, half),
                layers * half + rank_ref[layer * group + src],
            )
            return c

        lax.fori_loop(0, half, pick_step, 0)


def make_plan(old_slot, new_slot, group, slots):
    layers = old_slot.shape[0]
    half = group // 2
    smem = pl.BlockSpec(memory_space=pltpu.SMEM)
    i32 = lambda n: jax.ShapeDtypeStruct((n,), jnp.int32)
    return pl.pallas_call(
        functools.partial(plan_kernel, group, slots),
        out_shape=(i32(2 * layers), i32(layers * half), i32(layers * half), i32(1)),
        in_specs=[smem, smem],
        out_specs=(smem, smem, smem, smem),
        scratch_shapes=[pltpu.SMEM((layers * group,), jnp.int32)] * 3,
    )(old_slot, new_slot)


def move_kernel(
    dims, mine_ref, send_ref, pick_ref, master_ref, one_ref, two_ref, grad_ref,
    land0, land1, land2, clip_ref,
    src0, src1, src2, hub0, hub1, hub2, far0, far1, far2, out0, out1, out2, give0, give1, give2,
    norm_dp, norm_ex, norm_a, norm_b,
    a_send, a_recv, b_send, b_recv, c_send, c_recv, d_send, d_recv, e_send, e_recv,
):
    group, dps, layers, slots, rows, cols, tiles, piece, cap = dims
    half, hubs = group // 2, group // 4
    lands, srcs, hubbuf = (land0, land1, land2), (src0, src1, src2), (hub0, hub1, hub2)
    fars, outs, gives = (far0, far1, far2), (out0, out1, out2), (give0, give1, give2)
    me, my_dp = lax.axis_index("expert"), lax.axis_index("dp")
    my_half = lax.div(me, half)
    base = my_half * half
    spot = lax.rem(me, half)
    first_hub = hubs + my_half * hubs
    is_hub = (me >= hubs) & (me < 3 * hubs)
    my_piece = lax.rem(me, hubs)
    partner = jnp.where(my_half == 0, me + hubs, me - hubs)
    col_tiles = -(-cols // LANE)

    def place(ref, layer, block):
        for r in range(rows // SUB):
            for c in range(col_tiles):
                tile = block[r * SUB:(r + 1) * SUB, c * LANE:min((c + 1) * LANE, cols)]
                if tile.shape[1] < LANE:
                    tile = jnp.concatenate(
                        [tile, jnp.zeros((SUB, LANE - tile.shape[1]), jnp.float32)], axis=1
                    )
                ref[layer, r * col_tiles + c] = tile

    for layer in range(layers):
        place(src0, layer, master_ref[layer, mine_ref[layer]])
        for s in (src0, src1, src2):
            for t in range(tiles, piece * hubs):
                s[layer, t] = jnp.zeros((SUB, LANE), jnp.float32)

    barrier = pltpu.get_barrier_semaphore()

    def greet(d, c):
        @pl.when(d != me)
        def _():
            pl.semaphore_signal(barrier, inc=1, device_id={"expert": d}, device_id_type=MESH)

        return c

    def greet_dp(d, c):
        @pl.when(d != my_dp)
        def _():
            pl.semaphore_signal(barrier, inc=1, device_id={"dp": d}, device_id_type=MESH)

        return c

    lax.fori_loop(0, group, greet, 0)
    lax.fori_loop(0, dps, greet_dp, 0)
    pl.semaphore_wait(barrier, group + dps - 2)

    def a_copy(a, layer, p, slot):
        return pltpu.make_async_remote_copy(
            src_ref=srcs[a].at[layer, pl.ds(p * piece, piece)],
            dst_ref=hubbuf[a].at[layer * half + slot],
            send_sem=a_send.at[a, layer, p],
            recv_sem=a_recv.at[a, layer * half + slot],
            device_id={"expert": first_hub + p},
            device_id_type=MESH,
        )

    def a_start(a):
        for layer in range(layers):
            for p in range(hubs):
                mine = first_hub + p == me

                @pl.when(jnp.logical_not(mine))
                def _(layer=layer, p=p):
                    a_copy(a, layer, p, spot).start()

                @pl.when(mine)
                def _(layer=layer, p=p):
                    hubbuf[a][layer * half + spot] = srcs[a][layer, p * piece:(p + 1) * piece]

    def a_wait_send(a):
        for layer in range(layers):
            for p in range(hubs):

                @pl.when(first_hub + p != me)
                def _(layer=layer, p=p):
                    a_copy(a, layer, p, spot).wait_send()

    def a_wait_recv(a):
        for layer in range(layers):

            def step(j, c, layer=layer):
                @pl.when(j != spot)
                def _():
                    a_copy(a, layer, 0, j).wait_recv()

                return c

            lax.fori_loop(0, half, step, 0)

    def b_copy(a):
        return pltpu.make_async_remote_copy(
            src_ref=outs[a], dst_ref=fars[a], send_sem=b_send.at[a], recv_sem=b_recv.at[a],
            device_id={"expert": partner}, device_id_type=MESH,
        )

    def b_start(a):
        def step(k, c):
            outs[a][k] = hubbuf[a][send_ref[k]]
            return c

        lax.fori_loop(0, cap, step, 0)
        b_copy(a).start()

    def c_copy(a, layer, j, p):
        return pltpu.make_async_remote_copy(
            src_ref=gives[a].at[layer * half + j],
            dst_ref=lands[a].at[layer, pl.ds(p * piece, piece)],
            send_sem=c_send.at[a, layer * half + j],
            recv_sem=c_recv.at[a, layer, p],
            device_id={"expert": base + j},
            device_id_type=MESH,
        )

    def c_start(a):
        for layer in range(layers):

            def step(j, c, layer=layer):
                code = pick_ref[layer * half + j]
                near = hubbuf[a][jnp.minimum(code, layers * half - 1)]
                far = fars[a][jnp.clip(code - layers * half, 0, cap - 1)]
                chosen = jnp.where(code < layers * half, near, far)

                @pl.when(j != spot)
                def _():
                    gives[a][layer * half + j] = chosen
                    c_copy(a, layer, j, my_piece).start()

                @pl.when(j == spot)
                def _():
                    lands[a][layer, pl.ds(my_piece * piece, piece)] = chosen

                return c

            lax.fori_loop(0, half, step, 0)

    def c_wait_send(a):
        for layer in range(layers):

            def step(j, c, layer=layer):
                @pl.when(j != spot)
                def _():
                    c_copy(a, layer, j, my_piece).wait_send()

                return c

            lax.fori_loop(0, half, step, 0)

    def c_wait_recv(a):
        for layer in range(layers):
            for p in range(hubs):

                @pl.when(first_hub + p != me)
                def _(layer=layer, p=p):
                    c_copy(a, layer, 0, p).wait_recv()

    a_start(0)

    acc = jnp.zeros((rows, cols), jnp.float32)
    for layer in range(layers):
        for s in range(slots):
            wide = grad_ref[layer, s].astype(jnp.float32)
            acc = acc + wide * wide

    def exchange(value, send_buf, box, axis, size, mine, send_sem, recv_sem):
        tile = jnp.full((SUB, LANE), value, jnp.float32)
        send_buf[...] = tile
        box[mine] = tile

        def copy(peer, slot):
            return pltpu.make_async_remote_copy(
                src_ref=send_buf, dst_ref=box.at[slot], send_sem=send_sem.at[peer],
                recv_sem=recv_sem.at[slot], device_id={axis: peer}, device_id_type=MESH,
            )

        def each(act):
            def step(d, c):
                @pl.when(d != mine)
                def _():
                    act(d)

                return c

            lax.fori_loop(0, size, step, 0)

        each(lambda d: copy(d, mine).start())
        each(lambda d: copy(d, d).wait_recv())
        each(lambda d: copy(d, mine).wait_send())
        total = box[0]
        for d in range(1, size):
            total = total + box[d]
        return total

    by_dp = exchange(jnp.sum(acc), norm_a, norm_dp, "dp", dps, my_dp, d_send, d_recv)
    total = exchange(by_dp, norm_b, norm_ex, "expert", group, me, e_send, e_recv)
    entry_count = layers * slots * group * rows * dps * cols
    clip = jnp.minimum(1.0, CLIP_RMS * math.sqrt(entry_count) / (jnp.sqrt(total) + 1e-06))
    clip_ref[...] = clip
    scale = clip[0:1, 0:1]
    for layer in range(layers):
        slot = mine_ref[layer]
        first, second = moments(
            one_ref[layer, slot], two_ref[layer, slot],
            grad_ref[layer, slot].astype(jnp.float32), scale,
        )
        place(src1, layer, first)
        place(src2, layer, second)
    a_start(1)
    a_start(2)

    @pl.when(is_hub)
    def _():
        a_wait_recv(0)
        b_start(0)
        a_wait_recv(1)
        b_start(1)
        b_copy(0).wait_recv()
        c_start(0)
        a_wait_recv(2)
        b_start(2)
        b_copy(1).wait_recv()
        c_start(1)
        b_copy(2).wait_recv()
        c_start(2)
        for a in range(3):
            b_copy(a).wait_send()
            c_wait_send(a)

    for a in range(3):
        a_wait_send(a)
        c_wait_recv(a)


def move_blocks(plan, master, moment_one, moment_two, gradient, group, dps, cap):
    mine, send, pick = plan
    layers, slots, rows, cols = master.shape
    half, hubs = group // 2, group // 4
    tiles = (rows // SUB) * -(-cols // LANE)
    piece = -(-tiles // hubs)
    dims = (group, dps, layers, slots, rows, cols, tiles, piece, cap)
    smem = pl.BlockSpec(memory_space=pltpu.SMEM)
    vmem = pl.BlockSpec(memory_space=pltpu.VMEM)
    f32 = jnp.float32
    buf = lambda *lead: pltpu.VMEM(lead + (SUB, LANE), f32)
    dma = lambda *shape: pltpu.SemaphoreType.DMA(shape)
    land = jax.ShapeDtypeStruct((layers, piece * hubs, SUB, LANE), f32)
    return pl.pallas_call(
        functools.partial(move_kernel, dims),
        out_shape=(land, land, land, jax.ShapeDtypeStruct((SUB, LANE), f32)),
        in_specs=[smem] * 3 + [vmem] * 4,
        out_specs=(vmem,) * 4,
        scratch_shapes=[buf(layers, piece * hubs)] * 3
        + [buf(layers * half, piece)] * 3
        + [buf(cap, piece)] * 3
        + [buf(cap, piece)] * 3
        + [buf(layers * half, piece)] * 3
        + [buf(dps), buf(group), buf(), buf()]
        + [dma(3, layers, hubs), dma(3, layers * half), dma(3), dma(3), dma(3, layers * half),
           dma(3, layers, hubs), dma(dps), dma(dps), dma(group), dma(group)],
        compiler_params=pltpu.CompilerParams(
            collective_id=cap, has_side_effects=True, vmem_limit_bytes=48 * 1024 * 1024
        ),
    )(mine, send, pick, master, moment_one, moment_two, gradient)


def merge_kernel(mine_ref, master_ref, one_ref, two_ref, grad_ref, land0, land1, land2, clip_ref, w_ref, f_ref, s_ref):
    layer, slot = pl.program_id(0), pl.program_id(1)
    layers = pl.num_programs(0)
    rows, cols = w_ref.shape[2:]
    arrives = mine_ref[layers + layer] == slot

    @pl.when(jnp.logical_not(arrives))
    def _():
        first, second = moments(
            one_ref[0, 0], two_ref[0, 0], grad_ref[0, 0].astype(jnp.float32), clip_ref[0:1, 0:1]
        )
        f_ref[0, 0] = first
        s_ref[0, 0] = second
        w_ref[0, 0] = weights_of(master_ref[0, 0], first, second)

    @pl.when(arrives)
    def _():
        col_tiles = -(-cols // LANE)
        for r in range(rows // SUB):
            for c in range(col_tiles):
                t = r * col_tiles + c
                width = min(LANE, cols - c * LANE)
                at = (0, 0, pl.ds(r * SUB, SUB), pl.ds(c * LANE, width))
                first, second = land1[0, t][:, :width], land2[0, t][:, :width]
                f_ref[at] = first
                s_ref[at] = second
                w_ref[at] = weights_of(land0[0, t][:, :width], first, second)


def merge(mine, master, moment_one, moment_two, gradient, landed, clip):
    layers, slots, rows, cols = master.shape
    own = pl.BlockSpec((1, 1, rows, cols), lambda l, s, m: (l, s, 0, 0))
    came = pl.BlockSpec((1,) + landed[0].shape[1:], lambda l, s, m: (l, 0, 0, 0))
    out = jax.ShapeDtypeStruct(master.shape, jnp.float32)
    return pl.pallas_call(
        merge_kernel,
        out_shape=(out, out, out),
        grid_spec=pltpu.PrefetchScalarGridSpec(
            num_scalar_prefetch=1,
            grid=(layers, slots),
            in_specs=[own] * 4 + [came] * 3 + [pl.BlockSpec((SUB, LANE), lambda l, s, m: (0, 0))],
            out_specs=(own, own, own),
        ),
    )(mine, master, moment_one, moment_two, gradient, *landed, clip)


def shards(group, dps, master, moment_one, moment_two, gradient, old_slot, new_slot):
    layers, slots = master.shape[:2]
    mine, send, pick, count = make_plan(old_slot, new_slot, group, slots)
    *landed, clip = move_blocks(
        (mine, send, pick), master, moment_one, moment_two, gradient, group, dps, layers * (group // 2)
    )
    return merge(mine, master, moment_one, moment_two, gradient, landed, clip)


def solution(mesh):
    split = P(None, "expert", "dp", None)
    body = functools.partial(shards, mesh.shape["expert"], mesh.shape["dp"])
    return jax.shard_map(
        body, mesh=mesh, in_specs=(split,) * 4 + (P(), P()), out_specs=(split,) * 3, check_vma=False
    )
```

time: 241 us -> 99.6 us (0.41)
  Pallas kernels: 0 us -> 89.3 us
  blocking collectives: 85.5 us -> 0 us
  local copies, waits for them, and re-layouts: 62.5 us -> 8.68 us
  waiting for transfers between devices: 50.6 us -> 0 us
  other arithmetic: 21.8 us -> 0 us
  starting transfers between devices: 17.4 us -> 0 us
    pallas_call x0 -> x3, Pallas kernels: none -> 89.3 us  [the longest x1 77.8 us: move_blocks(): pl.pallas_call(functools.partial(move_kernel, dims), out_shape=(land, lan...]
    all_to_all x5 -> x0, waiting for transfers between devices: 50.6 us -> none  [the longest x3 28.6 us: relocate(): lax.all_to_all(packed, 'expert', split_axis=2, concat_axis=2, tiled=True)]
    all_to_all x3 -> x0, blocking collectives: 46.9 us -> none  [the longest x2 28.7 us: relocate(): lax.all_to_all(regrouped, 'expert', split_axis=2, concat_axis=2, tiled=True)]
    gather x30 -> x0, local copies, waits for them, and re-layouts: 41 us -> none  [the longest x18 36.5 us: pick_rows(): jnp.take(layer_block, layer_pick, axis=0)]
    psum x1 -> x0, blocking collectives: 38.7 us -> none  [grad_total(): return lax.psum(jnp.sum(gradient * gradient), ('dp', 'expert'))]
    reshape x18 -> x0, local copies, waits for them, and re-layouts: 19.3 us -> none  [the longest x4 10.5 us: relocate(): pick_rows(member.reshape(layer_count, capacity, flat_size), my_rank)]
    all_to_all x5 -> x0, starting transfers between devices: 17.4 us -> none  [the longest x3 10.5 us: relocate(): lax.all_to_all(packed, 'expert', split_axis=2, concat_axis=2, tiled=True)]
    select_n x4 -> x0, other arithmetic: 8.51 us -> none  [the longest x2 8.49 us: pick_rows(): jnp.take(layer_block, layer_pick, axis=0)]
  transfers between devices with their start and end apart: 5 -> 0, of which waited for: 5 -> 0; matrix products, arithmetic and copies ran while one was open for 4% -> 0% of each run, Pallas kernels for 0% -> 0%
where the time goes in v1:
time: 99.6 us; the launch traced here: 98.7 us
  Pallas kernels  89.3 us (90%)
  local copies, waits for them, and re-layouts  8.68 us (9%)
    pallas_call x1, Pallas kernels, move_blocks(): pl.pallas_call(functools.partial(move_kernel, dims), out_shape=(land, lan...  77.8 us
    pallas_call x1, Pallas kernels, merge(): pl.pallas_call(merge_kernel, out_shape=(out, out, out), grid_spec=pltpu.P...  8.97 us
    unnamed x20, local copies, waits for them, and re-layouts  8.68 us
    pallas_call x1, Pallas kernels, make_plan(): pl.pallas_call(functools.partial(plan_kernel, group, slots), out_shape=(i...  2.58 us

profile of v1, /device:TPU:0, one launch (start us, length us, event | category | flops | bytes accessed | tf_op | source)
XLA Modules:
  0.0 98.7 jit_solution(12317269054908426137)
XLA Ops:
  0.6 2.6 %shard_map.85 = (s32[4]{0:T(128)}, s32[8]{0:T(128)}, s32[8]{0:T(128)}, s32[1]{0:T(128)}) custom-call(s32[2,32]{1,0:T(2,128)} %old_ref.1, s32[2,32]{1,0:T(2,128)} %new_ref.1), custom_call_target="tpu_custom_call" | custom-call | tf_op jit(solution)/shard_map/pallas_call | solution.py:105
  3.2 0.0 copy-start
  3.2 1.4 %copy-done = f32[2,4,16,2880]{3,2,1,0:T(8,128)S(1)} copy-done((f32[2,4,16,2880]{3,2,1,0:T(8,128)S(1)}, f32[2,4,16,2880]{3,2,1,0:T(8,128)}, u32[]{:S(2)}) %copy-start) | copy-done | bytes 1474584
  4.6 0.0 copy-start.1
  4.6 1.4 %copy-done.1 = f32[2,4,16,2880]{3,2,1,0:T(8,128)S(1)} copy-done((f32[2,4,16,2880]{3,2,1,0:T(8,128)S(1)}, f32[2,4,16,2880]{3,2,1,0:T(8,128)}, u32[]{:S(2)}) %copy-start.1) | copy-done | bytes 1474584
  6.0 0.0 copy-start.2
  6.0 1.1 %copy-done.2 = bf16[2,4,16,2880]{3,2,1,0:T(8,128)(2,1)S(1)} copy-done((bf16[2,4,16,2880]{3,2,1,0:T(8,128)(2,1)S(1)}, bf16[2,4,16,2880]{3,2,1,0:T(8,128)(2,1)}, u32[]{:S(2)}) %copy-start.2) | copy-done | bytes 737304
  7.1 0.0 copy-start.7
  7.1 0.7 copy-done.7
  7.8 0.0 copy-start.8
  7.8 0.7 copy-done.8
  8.4 0.0 copy-start.9
  8.4 0.7 copy-done.9
  9.1 77.8 %shard_map.86 = (f32[2,46,8,128]{3,2,1,0:T(8,128)S(1)}, f32[2,46,8,128]{3,2,1,0:T(8,128)S(1)}, f32[2,46,8,128]{3,2,1,0:T(8,128)S(1)}, f32[8,128]{1,0:T(8,128)S(1)}) custom-call(s32[4]{0:T(128)S(1)} %copy-done.7, s32[8]{0:T(128)S(1)} %copy-done.8, s32[8]{0:T(128)S(1)} %copy-done.9, f32[2,4,16,2880]{3,2,1,0:T(8,128)S(1)} %copy-done, ...), custom_call_target="tpu_custom_call" | custom-call | tf_op jit(solution)/shard_map/pallas_call | solution.py:370
  86.9 0.0 copy-start.3
  86.9 0.7 copy-done.3
  87.6 0.0 copy-start.4
  87.6 0.7 copy-done.4
  88.3 0.0 copy-start.5
  88.3 0.8 copy-done.5
  89.1 0.0 copy-start.6
  89.1 0.6 copy-done.6
  89.7 9.0 %shard_map.87 = (f32[2,4,16,2880]{3,2,1,0:T(8,128)}, f32[2,4,16,2880]{3,2,1,0:T(8,128)}, f32[2,4,16,2880]{3,2,1,0:T(8,128)}) custom-call(s32[4]{0:T(128)} %get-tuple-element.10.mine_ref, f32[2,4,16,2880]{3,2,1,0:T(8,128)} %master_ref.3, f32[2,4,16,2880]{3,2,1,0:T(8,128)} %one_ref.3, f32[2,4,16,2880]{3,2,1,0:T(8,128)} %two_ref.3, ...), custom_call_target="tpu_custom_call" | custom-call | tf_op jit(solution)/shard_map/pallas_call | solution.py:423
Async XLA Ops:
  3.2 1.4 %copy-start = (f32[2,4,16,2880]{3,2,1,0:T(8,128)S(1)}, f32[2,4,16,2880]{3,2,1,0:T(8,128)}, u32[]{:S(2)}) copy-start(f32[2,4,16,2880]{3,2,1,0:T(8,128)} %master_ref.3) | copy-start | bytes 4423684
  4.6 1.4 %copy-start.1 = (f32[2,4,16,2880]{3,2,1,0:T(8,128)S(1)}, f32[2,4,16,2880]{3,2,1,0:T(8,128)}, u32[]{:S(2)}) copy-start(f32[2,4,16,2880]{3,2,1,0:T(8,128)} %one_ref.3) | copy-start | bytes 4423684
  6.0 1.1 %copy-start.2 = (bf16[2,4,16,2880]{3,2,1,0:T(8,128)(2,1)S(1)}, bf16[2,4,16,2880]{3,2,1,0:T(8,128)(2,1)}, u32[]{:S(2)}) copy-start(bf16[2,4,16,2880]{3,2,1,0:T(8,128)(2,1)} %grad_ref.3) | copy-start | bytes 2211844
  7.1 0.7 copy-start.7
  7.8 0.7 copy-start.8
  8.4 0.7 copy-start.9
  86.9 0.7 copy-start.3
  87.6 0.7 copy-start.4
  88.3 0.8 copy-start.5
  89.1 0.6 copy-start.6

commit v2 on v1

v2 whole, which is shorter than its diff:
```python
import functools
import math

import jax
import jax.numpy as jnp
from jax import lax
from jax.experimental import pallas as pl
from jax.experimental.pallas import tpu as pltpu
from jax.sharding import PartitionSpec as P

MESH = pl.DeviceIdType.MESH
BETA_ONE = 0.9
BETA_TWO = 0.95
LEARN_RATE = 0.05
DECAY_RATE = 0.1
ADAM_EPS = 1e-08
CLIP_RMS = 2.0
FIRST_FIX = 1.0 - 0.9**10
SECOND_FIX = 1.0 - 0.95**10
SUB, LANE = 8, 128


def moments(moment_one, moment_two, gradient, clip_scale):
    scaled = gradient * clip_scale
    first_moment = BETA_ONE * moment_one + (1.0 - BETA_ONE) * scaled
    second = BETA_TWO * moment_two + (1.0 - BETA_TWO) * scaled * scaled
    return first_moment, second


def weights_of(master, first_moment, second):
    step_dir = first_moment / FIRST_FIX / (jnp.sqrt(second / SECOND_FIX) + ADAM_EPS)
    return master - LEARN_RATE * (step_dir + DECAY_RATE * master)


def plan_kernel(group, slots, levels, old_ref, new_ref, mine_ref, send_ref, pick_ref, count_ref, dst_ref, src_ref, rank_ref):
    layers, experts = old_ref.shape
    half = group // 2
    me = lax.axis_index("expert")
    my_half = lax.div(me, half)

    def clear(i, c):
        send_ref[i] = 0
        return c

    lax.fori_loop(0, layers * half, clear, 0)
    for layer in range(layers):

        def expert_step(e, c):
            old, new = old_ref[layer, e], new_ref[layer, e]

            @pl.when(old != new)
            def _():
                src, dst = lax.div(old, slots), lax.div(new, slots)
                dst_ref[layer * group + src] = dst
                src_ref[layer * group + dst] = src

                @pl.when(src == me)
                def _():
                    mine_ref[layer] = lax.rem(old, slots)

                @pl.when(dst == me)
                def _():
                    mine_ref[layers + layer] = lax.rem(new, slots)

            return c

        lax.fori_loop(0, experts, expert_step, 0)
    counts = [jnp.int32(0), jnp.int32(0)]
    for layer in range(layers):
        for side in range(2):

            def rank_step(j, count, side=side):
                at = layer * group + side * half + j
                crosses = lax.div(dst_ref[at], half) != side
                rank_ref[at] = count

                @pl.when(crosses & (my_half == side))
                def _():
                    send_ref[count] = layer * half + j

                return count + crosses.astype(jnp.int32)

            counts[side] = lax.fori_loop(0, half, rank_step, counts[side])
    count_ref[0] = sum((counts[0] > level).astype(jnp.int32) for level in levels[:-1])
    for layer in range(layers):

        def pick_step(j, c):
            src = src_ref[layer * group + my_half * half + j]
            local = lax.div(src, half) == my_half
            pick_ref[layer * half + j] = jnp.where(
                local,
                layer * half + lax.rem(src, half),
                layers * half + rank_ref[layer * group + src],
            )
            return c

        lax.fori_loop(0, half, pick_step, 0)


def make_plan(old_slot, new_slot, group, slots, levels):
    layers = old_slot.shape[0]
    half = group // 2
    smem = pl.BlockSpec(memory_space=pltpu.SMEM)
    i32 = lambda n: jax.ShapeDtypeStruct((n,), jnp.int32)
    return pl.pallas_call(
        functools.partial(plan_kernel, group, slots, levels),
        out_shape=(i32(2 * layers), i32(layers * half), i32(layers * half), i32(1)),
        in_specs=[smem, smem],
        out_specs=(smem, smem, smem, smem),
        scratch_shapes=[pltpu.SMEM((layers * group,), jnp.int32)] * 3,
    )(old_slot, new_slot)


def move_kernel(
    dims, mine_ref, send_ref, pick_ref, master_hbm, one_hbm, two_hbm, grad_hbm,
    land0, land1, land2, clip_ref, master_ref, one_ref, two_ref, grad_ref, src0, src1, src2,
    norm_dp, norm_ex, norm_a, norm_b, in_sem,
    a_send, a_recv, b_send, b_recv, c_send, c_recv, d_send, d_recv, e_send, e_recv, *bufs,
):
    group, dps, layers, slots, rows, cols, tiles, cuts, cap = dims
    half, hubs = group // 2, group // 4
    piece = cuts[-1]
    chunks = [(a, lo, hi) for a in range(3) for lo, hi in zip(cuts[:-1], cuts[1:])]
    count = len(chunks)
    hubbuf, fars, outs, gives = (bufs[i * count:(i + 1) * count] for i in range(4))
    lands, srcs = (land0, land1, land2), (src0, src1, src2)
    me, my_dp = lax.axis_index("expert"), lax.axis_index("dp")
    my_half = lax.div(me, half)
    base = my_half * half
    spot = lax.rem(me, half)
    first_hub = hubs + my_half * hubs
    is_hub = (me >= hubs) & (me < 3 * hubs)
    my_piece = lax.rem(me, hubs)
    partner = jnp.where(my_half == 0, me + hubs, me - hubs)
    col_tiles = -(-cols // LANE)

    loads = [
        pltpu.make_async_copy(src, dst, in_sem.at[i])
        for i, (src, dst) in enumerate(
            ((master_hbm, master_ref), (grad_hbm, grad_ref), (one_hbm, one_ref), (two_hbm, two_ref))
        )
    ]
    for load in loads:
        load.start()

    barrier = pltpu.get_barrier_semaphore()

    def greet(d, c):
        @pl.when(d != me)
        def _():
            pl.semaphore_signal(barrier, inc=1, device_id={"expert": d}, device_id_type=MESH)

        return c

    def greet_dp(d, c):
        @pl.when(d != my_dp)
        def _():
            pl.semaphore_signal(barrier, inc=1, device_id={"dp": d}, device_id_type=MESH)

        return c

    lax.fori_loop(0, group, greet, 0)
    lax.fori_loop(0, dps, greet_dp, 0)

    def padded(tile):
        if tile.shape[1] == LANE:
            return tile
        return jnp.concatenate([tile, jnp.zeros((SUB, LANE - tile.shape[1]), jnp.float32)], axis=1)

    def spans():
        for r in range(rows // SUB):
            for c in range(col_tiles):
                yield r * col_tiles + c, pl.ds(r * SUB, SUB), pl.ds(c * LANE, min(LANE, cols - c * LANE))

    loads[0].wait()
    for layer in range(layers):
        slot = mine_ref[layer]
        for t, rspan, cspan in spans():
            src0[layer, t] = padded(master_ref[layer, slot, rspan, cspan])
        for s in srcs:
            for t in range(tiles, piece * hubs):
                s[layer, t] = jnp.zeros((SUB, LANE), jnp.float32)

    pl.semaphore_wait(barrier, group + dps - 2)

    def a_copy(n, layer, p, slot):
        a, lo, hi = chunks[n]
        return pltpu.make_async_remote_copy(
            src_ref=srcs[a].at[layer, pl.ds(p * piece + lo, hi - lo)],
            dst_ref=hubbuf[n].at[layer * half + slot],
            send_sem=a_send.at[n, layer, p],
            recv_sem=a_recv.at[n, layer * half + slot],
            device_id={"expert": first_hub + p},
            device_id_type=MESH,
        )

    def a_start(n):
        a, lo, hi = chunks[n]
        for layer in range(layers):
            for p in range(hubs):
                mine = first_hub + p == me

                @pl.when(jnp.logical_not(mine))
                def _(layer=layer, p=p):
                    a_copy(n, layer, p, spot).start()

                @pl.when(mine)
                def _(layer=layer, p=p):
                    hubbuf[n][layer * half + spot] = srcs[a][layer, p * piece + lo:p * piece + hi]

    def a_wait_send(n):
        for layer in range(layers):
            for p in range(hubs):

                @pl.when(first_hub + p != me)
                def _(layer=layer, p=p):
                    a_copy(n, layer, p, spot).wait_send()

    def a_wait_recv(n):
        for layer in range(layers):

            def step(j, c, layer=layer):
                @pl.when(j != spot)
                def _():
                    a_copy(n, layer, 0, j).wait_recv()

                return c

            lax.fori_loop(0, half, step, 0)

    def b_copy(n):
        return pltpu.make_async_remote_copy(
            src_ref=outs[n], dst_ref=fars[n], send_sem=b_send.at[n], recv_sem=b_recv.at[n],
            device_id={"expert": partner}, device_id_type=MESH,
        )

    def b_start(n):
        def step(k, c):
            outs[n][k] = hubbuf[n][send_ref[k]]
            return c

        lax.fori_loop(0, cap, step, 0)
        b_copy(n).start()

    def landing(n, layer, p):
        a, lo, hi = chunks[n]
        return lands[a].at[layer, pl.ds(p * piece + lo, hi - lo)]

    def c_copy(n, layer, j, p):
        return pltpu.make_async_remote_copy(
            src_ref=gives[n].at[layer * half + j],
            dst_ref=landing(n, layer, p),
            send_sem=c_send.at[n, layer * half + j],
            recv_sem=c_recv.at[n, layer, p],
            device_id={"expert": base + j},
            device_id_type=MESH,
        )

    def c_start(n):
        for layer in range(layers):

            def step(j, c, layer=layer):
                code = pick_ref[layer * half + j]
                near = hubbuf[n][jnp.minimum(code, layers * half - 1)]
                far = fars[n][jnp.clip(code - layers * half, 0, cap - 1)]
                gives[n][layer * half + j] = jnp.where(code < layers * half, near, far)
                return c

            lax.fori_loop(0, half, step, 0)

        for layer in range(layers):

            def send(j, c, layer=layer):
                @pl.when(j != spot)
                def _():
                    c_copy(n, layer, j, my_piece).start()

                return c

            lax.fori_loop(0, half, send, 0)
            landing(n, layer, my_piece)[...] = gives[n][layer * half + spot]

    def c_wait_send(n):
        for layer in range(layers):

            def step(j, c, layer=layer):
                @pl.when(j != spot)
                def _():
                    c_copy(n, layer, j, my_piece).wait_send()

                return c

            lax.fori_loop(0, half, step, 0)

    def c_wait_recv(n):
        for layer in range(layers):
            for p in range(hubs):

                @pl.when(first_hub + p != me)
                def _(layer=layer, p=p):
                    c_copy(n, layer, 0, p).wait_recv()

    early = [n for n in range(count) if chunks[n][0] == 0]
    for n in early:
        a_start(n)

    loads[1].wait()
    parts = [jnp.zeros((rows, LANE), jnp.float32) for _ in range(4)]
    tails = jnp.zeros((rows, cols - (col_tiles - 1) * LANE), jnp.float32)
    for layer in range(layers):
        for s in range(slots):
            for c in range(col_tiles - 1):
                wide = grad_ref[layer, s, :, pl.ds(c * LANE, LANE)].astype(jnp.float32)
                parts[c % 4] = parts[c % 4] + wide * wide
            last = (col_tiles - 1) * LANE
            wide = grad_ref[layer, s, :, pl.ds(last, cols - last)].astype(jnp.float32)
            tails = tails + wide * wide
    square = jnp.sum((parts[0] + parts[1]) + (parts[2] + parts[3])) + jnp.sum(tails)

    def exchange(value, send_buf, box, axis, size, mine, send_sem, recv_sem):
        tile = jnp.full((SUB, LANE), value, jnp.float32)
        send_buf[...] = tile
        box[mine] = tile

        def copy(peer, slot):
            return pltpu.make_async_remote_copy(
                src_ref=send_buf, dst_ref=box.at[slot], send_sem=send_sem.at[peer],
                recv_sem=recv_sem.at[slot], device_id={axis: peer}, device_id_type=MESH,
            )

        def each(act):
            def step(d, c):
                @pl.when(d != mine)
                def _():
                    act(d)

                return c

            lax.fori_loop(0, size, step, 0)

        each(lambda d: copy(d, mine).start())
        each(lambda d: copy(d, d).wait_recv())
        each(lambda d: copy(d, mine).wait_send())
        total = box[0]
        for d in range(1, size):
            total = total + box[d]
        return total

    by_dp = exchange(square, norm_a, norm_dp, "dp", dps, my_dp, d_send, d_recv)
    total = exchange(by_dp, norm_b, norm_ex, "expert", group, me, e_send, e_recv)
    entry_count = layers * slots * group * rows * dps * cols
    clip = jnp.minimum(1.0, CLIP_RMS * math.sqrt(entry_count) / (jnp.sqrt(total) + 1e-06))
    clip_ref[...] = clip
    loads[2].wait()
    loads[3].wait()
    for layer in range(layers):
        slot = mine_ref[layer]
        for c in range(col_tiles):
            cspan = pl.ds(c * LANE, min(LANE, cols - c * LANE))
            wide = grad_ref[layer, slot, :, cspan].astype(jnp.float32)
            first, second = moments(
                one_ref[layer, slot, :, cspan], two_ref[layer, slot, :, cspan], wide, clip[0:1, 0:1]
            )
            for r in range(rows // SUB):
                src1[layer, r * col_tiles + c] = padded(first[r * SUB:(r + 1) * SUB])
                src2[layer, r * col_tiles + c] = padded(second[r * SUB:(r + 1) * SUB])
    for n in range(len(early), count):
        a_start(n)

    @pl.when(is_hub)
    def _():
        for n in range(count):
            a_wait_recv(n)
            b_start(n)
            if n:
                b_copy(n - 1).wait_recv()
                c_start(n - 1)
        b_copy(count - 1).wait_recv()
        c_start(count - 1)
        for n in range(count):
            b_copy(n).wait_send()
            c_wait_send(n)

    for n in range(count):
        a_wait_send(n)
        c_wait_recv(n)


def move_blocks(group, dps, cap, ident, mine, send, pick, master, moment_one, moment_two, gradient):
    layers, slots, rows, cols = master.shape
    half, hubs = group // 2, group // 4
    tiles = (rows // SUB) * -(-cols // LANE)
    piece = -(-tiles // hubs)
    cuts = (0, piece // 2, piece)
    dims = (group, dps, layers, slots, rows, cols, tiles, cuts, cap)
    smem = pl.BlockSpec(memory_space=pltpu.SMEM)
    hbm = pl.BlockSpec(memory_space=pltpu.HBM)
    vmem = pl.BlockSpec(memory_space=pltpu.VMEM)
    f32 = jnp.float32
    buf = lambda *lead: pltpu.VMEM(lead + (SUB, LANE), f32)
    dma = lambda *shape: pltpu.SemaphoreType.DMA(shape)
    land = jax.ShapeDtypeStruct((layers, piece * hubs, SUB, LANE), f32)
    widths = [hi - lo for lo, hi in zip(cuts[:-1], cuts[1:])] * 3
    count = len(widths)
    return pl.pallas_call(
        functools.partial(move_kernel, dims),
        out_shape=(land, land, land, jax.ShapeDtypeStruct((SUB, LANE), f32)),
        in_specs=[smem] * 3 + [hbm] * 4,
        out_specs=(vmem,) * 4,
        scratch_shapes=[pltpu.VMEM(master.shape, f32)] * 3
        + [pltpu.VMEM(gradient.shape, gradient.dtype)]
        + [buf(layers, piece * hubs)] * 3
        + [buf(dps), buf(group), buf(), buf()]
        + [dma(4)]
        + [dma(count, layers, hubs), dma(count, layers * half), dma(count), dma(count),
           dma(count, layers * half), dma(count, layers, hubs), dma(dps), dma(dps), dma(group), dma(group)]
        + [buf(layers * half, w) for w in widths]
        + [buf(cap, w) for w in widths] * 2
        + [buf(layers * half, w) for w in widths],
        compiler_params=pltpu.CompilerParams(
            collective_id=ident, has_side_effects=True, vmem_limit_bytes=40 * 1024 * 1024
        ),
    )(mine, send, pick, master, moment_one, moment_two, gradient)


def merge_kernel(
    mine_ref, master_hbm, one_hbm, two_hbm, grad_hbm, came0, came1, came2, clip_ref, w_hbm, f_hbm, s_hbm,
    master_ref, one_ref, two_ref, grad_ref, w_ref, f_ref, s_ref, in_sem, out_sem,
):
    layers, slots, rows, cols = master_ref.shape
    col_tiles = -(-cols // LANE)
    pairs = ((grad_hbm, grad_ref), (one_hbm, one_ref), (two_hbm, two_ref), (master_hbm, master_ref))
    blocks = layers * slots

    def read(i, n):
        layer, slot = lax.div(i, slots), lax.rem(i, slots)
        src, dst = pairs[n]
        return pltpu.make_async_copy(src.at[layer, slot], dst.at[layer, slot], in_sem.at[i, n])

    def write(i, n):
        layer, slot = lax.div(i, slots), lax.rem(i, slots)
        src, dst = ((w_ref, w_hbm), (f_ref, f_hbm), (s_ref, s_hbm))[n]
        return pltpu.make_async_copy(src.at[layer, slot], dst.at[layer, slot], out_sem.at[i, n])

    def begin(i, c):
        for n in range(4):
            read(i, n).start()
        return c

    lax.fori_loop(0, blocks, begin, 0)

    def step(i, c):
        layer, slot = lax.div(i, slots), lax.rem(i, slots)
        for n in range(4):
            read(i, n).wait()

        arrives = mine_ref[layers + layer] == slot

        @pl.when(jnp.logical_not(arrives))
        def _():
            scale = clip_ref[0:1, 0:1]
            for k in range(col_tiles):
                at = (layer, slot, slice(None), pl.ds(k * LANE, min(LANE, cols - k * LANE)))
                first, second = moments(one_ref[at], two_ref[at], grad_ref[at].astype(jnp.float32), scale)
                f_ref[at] = first
                s_ref[at] = second
                w_ref[at] = weights_of(master_ref[at], first, second)

        @pl.when(arrives)
        def _():
            for r in range(rows // SUB):
                for k in range(col_tiles):
                    t = r * col_tiles + k
                    width = min(LANE, cols - k * LANE)
                    at = (layer, slot, pl.ds(r * SUB, SUB), pl.ds(k * LANE, width))
                    first, second = came1[layer, t][:, :width], came2[layer, t][:, :width]
                    f_ref[at] = first
                    s_ref[at] = second
                    w_ref[at] = weights_of(came0[layer, t][:, :width], first, second)

        for n in range(3):
            write(i, n).start()
        return c

    lax.fori_loop(0, blocks, step, 0)

    def end(i, c):
        for n in range(3):
            write(i, n).wait()
        return c

    lax.fori_loop(0, blocks, end, 0)


def merge(mine, master, moment_one, moment_two, gradient, landed, clip):
    layers, slots = master.shape[:2]
    blocks = layers * slots
    smem = pl.BlockSpec(memory_space=pltpu.SMEM)
    hbm = pl.BlockSpec(memory_space=pltpu.HBM)
    vmem = pl.BlockSpec(memory_space=pltpu.VMEM)
    full = pltpu.VMEM(master.shape, jnp.float32)
    out = jax.ShapeDtypeStruct(master.shape, jnp.float32)
    dma = lambda *shape: pltpu.SemaphoreType.DMA(shape)
    return pl.pallas_call(
        merge_kernel,
        out_shape=(out, out, out),
        in_specs=[smem] + [hbm] * 4 + [vmem] * 4,
        out_specs=(hbm,) * 3,
        scratch_shapes=[full] * 3
        + [pltpu.VMEM(gradient.shape, gradient.dtype)]
        + [full] * 3
        + [dma(blocks, 4), dma(blocks, 3)],
        compiler_params=pltpu.CompilerParams(vmem_limit_bytes=40 * 1024 * 1024),
    )(mine, master, moment_one, moment_two, gradient, *landed, clip)


def shards(group, dps, master, moment_one, moment_two, gradient, old_slot, new_slot):
    layers, slots = master.shape[:2]
    full = layers * (group // 2)
    levels = sorted({-(-full * step // 8) for step in range(1, 9)})
    mine, send, pick, index = make_plan(old_slot, new_slot, group, slots, levels)
    moves = [
        functools.partial(move_blocks, group, dps, level, ident) for ident, level in enumerate(levels)
    ]
    *landed, clip = lax.switch(
        index[0], moves, mine, send, pick, master, moment_one, moment_two, gradient
    )
    return merge(mine, master, moment_one, moment_two, gradient, landed, clip)


def solution(mesh):
    split = P(None, "expert", "dp", None)
    body = functools.partial(shards, mesh.shape["expert"], mesh.shape["dp"])
    return jax.shard_map(
        body, mesh=mesh, in_specs=(split,) * 4 + (P(), P()), out_specs=(split,) * 3, check_vma=False
    )
```

time: 99.6 us -> 59.1 us (0.59)
  Pallas kernels: 89.3 us -> 56.9 us
  local copies, waits for them, and re-layouts: 8.68 us -> 0 us
    pallas_call x1, Pallas kernels: 77.8 us -> 48.8 us  [move_blocks(): pl.pallas_call(functools.partial(move_kernel, dims), out_shape=(land, lan...]
    unnamed x20 -> x0, local copies, waits for them, and re-layouts: 8.68 us -> none
    pallas_call x2, Pallas kernels: 11.6 us -> 8.14 us  [the longest x1 5.47 us: merge(): pl.pallas_call(merge_kernel, out_shape=(out, out, out), in_specs=[smem] +...]
where the time goes in v2:
time: 59.1 us; the launch traced here: 58.2 us
  Pallas kernels  56.9 us (96%)
  between operations  1.3 us (2%)
    pallas_call x1, Pallas kernels, move_blocks(): pl.pallas_call(functools.partial(move_kernel, dims), out_shape=(land, lan...  48.8 us
    pallas_call x1, Pallas kernels, merge(): pl.pallas_call(merge_kernel, out_shape=(out, out, out), in_specs=[smem] +...  5.47 us
    pallas_call x1, Pallas kernels, make_plan(): pl.pallas_call(functools.partial(plan_kernel, group, slots, levels), out_...  2.66 us

profile of v2, /device:TPU:0, one launch (start us, length us, event | category | flops | bytes accessed | tf_op | source)
XLA Modules:
  0.0 58.2 jit_solution(15822813982761994201)
XLA Ops:
  0.6 2.7 %shard_map.85 = (s32[4]{0:T(128)S(1)}, s32[8]{0:T(128)S(1)}, s32[8]{0:T(128)S(1)}, s32[1]{0:T(128)}) custom-call(s32[2,32]{1,0:T(2,128)} %old_ref.1, s32[2,32]{1,0:T(2,128)} %new_ref.1), custom_call_target="tpu_custom_call" | custom-call | tf_op jit(solution)/shard_map/pallas_call | solution.py:105
  4.0 48.8 %conditional.1 = ((f32[2,46,8,128]{3,2,1,0:T(8,128)S(1)}, f32[2,46,8,128]{3,2,1,0:T(8,128)S(1)}, f32[2,46,8,128]{3,2,1,0:T(8,128)S(1)}, f32[8,128]{1,0:T(8,128)S(1)})) conditional(s32[]{:T(128)} %bitcast, (s32[4]{0:T(128)S(1)}, s32[8]{0:T(128)S(1)}, s32[8]{0:T(128)S(1)}, f32[2,4,16,2880]{3,2,1,0:T(8,128)}, ...), branch_computations={%region_0.0_spmd, %region_1.0_spmd, %region_2.0_spmd, %region_3.0_... | conditional | bytes 8 | solution.py:525
  4.0 48.8 %branch_2_fun.1 = (f32[2,46,8,128]{3,2,1,0:T(8,128)S(1)}, f32[2,46,8,128]{3,2,1,0:T(8,128)S(1)}, f32[2,46,8,128]{3,2,1,0:T(8,128)S(1)}, f32[8,128]{1,0:T(8,128)S(1)}) custom-call(s32[4]{0:T(128)S(1)} %get-tuple-element.126.mine_ref, s32[8]{0:T(128)S(1)} %get-tuple-element.127.send_ref, s32[8]{0:T(128)S(1)} %get-tuple-element.128.pick_ref, ...), custom_call_target="tpu_custom_call" | custom-call | tf_op jit(solution)/shard_map/cond/branch_2_fun/pallas_call | solution.py:405
  52.8 5.5 %shard_map.86 = (f32[2,4,16,2880]{3,2,1,0:T(8,128)}, f32[2,4,16,2880]{3,2,1,0:T(8,128)}, f32[2,4,16,2880]{3,2,1,0:T(8,128)}) custom-call(s32[4]{0:T(128)S(1)} %get-tuple-element.179.mine_ref, f32[2,4,16,2880]{3,2,1,0:T(8,128)} %master_hbm.1, f32[2,4,16,2880]{3,2,1,0:T(8,128)} %one_hbm.1, f32[2,4,16,2880]{3,2,1,0:T(8,128)} %two_hbm.1, ...), custom_call_target="tpu_custom_call" | custom-call | tf_op jit(solution)/shard_map/pallas_call | solution.py:504

commit v3 on v2

--- a/solution.py
+++ b/solution.py
@@ -391,7 +391,7 @@
     half, hubs = group // 2, group // 4
     tiles = (rows // SUB) * -(-cols // LANE)
     piece = -(-tiles // hubs)
-    cuts = (0, piece // 2, piece)
+    cuts = tuple(sorted({0, piece // 3, piece * 2 // 3, piece}))
     dims = (group, dps, layers, slots, rows, cols, tiles, cuts, cap)
     smem = pl.BlockSpec(memory_space=pltpu.SMEM)
     hbm = pl.BlockSpec(memory_space=pltpu.HBM)
@@ -517,7 +517,7 @@
 def shards(group, dps, master, moment_one, moment_two, gradient, old_slot, new_slot):
     layers, slots = master.shape[:2]
     full = layers * (group // 2)
-    levels = sorted({-(-full * step // 8) for step in range(1, 9)})
+    levels = sorted({-(-full * step // 8) for step in (3, 4, 5, 6, 8)})
     mine, send, pick, index = make_plan(old_slot, new_slot, group, slots, levels)
     moves = [
         functools.partial(move_blocks, group, dps, level, ident) for ident, level in enumerate(levels)

time: 59.1 us -> 65.3 us (1.10); the launches traced: 58.2 us -> 65.1 us
  Pallas kernels: 56.9 us -> 63.8 us
    pallas_call x1, Pallas kernels: 48.8 us -> 55.7 us  [move_blocks(): pl.pallas_call(functools.partial(move_kernel, dims), out_shape=(land, lan...]
where the time goes in v3:
time: 65.3 us; the launch traced here: 65.1 us
  Pallas kernels  63.8 us (98%)
  between operations  1.3 us (2%)
    pallas_call x1, Pallas kernels, move_blocks(): pl.pallas_call(functools.partial(move_kernel, dims), out_shape=(land, lan...  55.7 us
    pallas_call x1, Pallas kernels, merge(): pl.pallas_call(merge_kernel, out_shape=(out, out, out), in_specs=[smem] +...  5.47 us
    pallas_call x1, Pallas kernels, make_plan(): pl.pallas_call(functools.partial(plan_kernel, group, slots, levels), out_...  2.66 us

profile of v3, /device:TPU:0, one launch (start us, length us, event | category | flops | bytes accessed | tf_op | source)
XLA Modules:
  0.0 65.1 jit_solution(13454091544413867007)
XLA Ops:
  0.6 2.7 %shard_map.85 = (s32[4]{0:T(128)S(1)}, s32[8]{0:T(128)S(1)}, s32[8]{0:T(128)S(1)}, s32[1]{0:T(128)}) custom-call(s32[2,32]{1,0:T(2,128)} %old_ref.1, s32[2,32]{1,0:T(2,128)} %new_ref.1), custom_call_target="tpu_custom_call" | custom-call | tf_op jit(solution)/shard_map/pallas_call | solution.py:105
  3.9 55.7 %conditional.1 = ((f32[2,46,8,128]{3,2,1,0:T(8,128)S(1)}, f32[2,46,8,128]{3,2,1,0:T(8,128)S(1)}, f32[2,46,8,128]{3,2,1,0:T(8,128)S(1)}, f32[8,128]{1,0:T(8,128)S(1)})) conditional(s32[]{:T(128)} %bitcast, (s32[4]{0:T(128)S(1)}, s32[8]{0:T(128)S(1)}, s32[8]{0:T(128)S(1)}, f32[2,4,16,2880]{3,2,1,0:T(8,128)}, ...), branch_computations={%region_0.0_spmd, %region_1.0_spmd, %region_2.0_spmd, %region_3.0_... | conditional | bytes 8 | solution.py:525
  4.0 55.7 %branch_2_fun.1 = (f32[2,46,8,128]{3,2,1,0:T(8,128)S(1)}, f32[2,46,8,128]{3,2,1,0:T(8,128)S(1)}, f32[2,46,8,128]{3,2,1,0:T(8,128)S(1)}, f32[8,128]{1,0:T(8,128)S(1)}) custom-call(s32[4]{0:T(128)S(1)} %get-tuple-element.84.mine_ref, s32[8]{0:T(128)S(1)} %get-tuple-element.85.send_ref, s32[8]{0:T(128)S(1)} %get-tuple-element.86.pick_ref, ...), custom_call_target="tpu_custom_call" | custom-call | tf_op jit(solution)/shard_map/cond/branch_2_fun/pallas_call | solution.py:405
  59.7 5.5 %shard_map.86 = (f32[2,4,16,2880]{3,2,1,0:T(8,128)}, f32[2,4,16,2880]{3,2,1,0:T(8,128)}, f32[2,4,16,2880]{3,2,1,0:T(8,128)}) custom-call(s32[4]{0:T(128)S(1)} %get-tuple-element.116.mine_ref, f32[2,4,16,2880]{3,2,1,0:T(8,128)} %master_hbm.1, f32[2,4,16,2880]{3,2,1,0:T(8,128)} %one_hbm.1, f32[2,4,16,2880]{3,2,1,0:T(8,128)} %two_hbm.1, ...), custom_call_target="tpu_custom_call" | custom-call | tf_op jit(solution)/shard_map/pallas_call | solution.py:504
